TPU v7x, 128 devices: a whole 4x4x4 slice. The times are simulated.
128 devices in a mesh: dp: 1, tp: 2 (over core), cp: 64 (over z, y, x).
Axes of the slice: x: 4, y: 4, z: 4, core: 2. Of those that a mesh axis runs over, the one named last changes fastest.
Arguments:
- x: bfloat16 [16384, 4096], P(('dp', 'cp'))
- k_cache: bfloat16 [16384, 2, 128], P(('dp', 'cp'), 'tp')
- v_cache: bfloat16 [16384, 2, 128], P(('dp', 'cp'), 'tp')
- rope_table: float32 [16384, 64], P(('dp', 'cp'))
- norm_gain: bfloat16 [4096], replicated
- w_qkv: bfloat16 [4096, 4608], P(None, 'tp')
- b_qkv: bfloat16 [4608], P('tp')
- w_out: bfloat16 [4096, 4096], P('tp')
Outputs:
- output 1: bfloat16 [16384, 4096], P(('dp', 'cp'))
- output 2: bfloat16 [16384, 2, 128], P(('dp', 'cp'), 'tp')
- output 3: bfloat16 [16384, 2, 128], P(('dp', 'cp'), 'tp')
All inputs are finite; a program needn't handle non-finite values.
Results may differ from a plain program's by a relative error of at most 0.00350049.
Values are sent between devices in bfloat16 or wider.
A program may use at most 1 GiB of HBM per device.

v0:
```python
import jax
import jax.numpy as jnp
from jax import lax
from jax.sharding import PartitionSpec as P, NamedSharding

EPS = 1.5625e-07
MASK_VALUE = -1e30


def apply_rotary(vals, cos_t, sin_t):
    pair_count = cos_t.shape[-1]
    lead_shape = vals.shape[:-1]
    paired = vals[..., :2 * pair_count].reshape(lead_shape + (pair_count, 2))
    even_part = paired[..., 0]
    odd_part = paired[..., 1]
    turned = jnp.stack([even_part * cos_t - odd_part * sin_t, odd_part * cos_t + even_part * sin_t], axis=-1)
    return jnp.concatenate([turned.reshape(lead_shape + (2 * pair_count,)), vals[..., 2 * pair_count:]], axis=-1)


def project_new(x, rope_table, norm_gain, w_qkv, b_qkv, kv_count, head_dim):
    x_f32 = x.astype(jnp.float32)
    inv_rms = lax.rsqrt(jnp.mean(x_f32 * x_f32, axis=-1, keepdims=True) + EPS)
    hidden = (x_f32 * inv_rms * norm_gain.astype(jnp.float32)).astype(jnp.bfloat16)
    tok_rows = x.shape[0]
    group = w_qkv.shape[1] // (kv_count * head_dim) - 2
    qkv_all = jnp.dot(hidden, w_qkv, preferred_element_type=jnp.float32) + b_qkv.astype(jnp.float32)
    qkv_all = qkv_all.reshape(tok_rows, kv_count, group + 2, head_dim)
    pair_count = rope_table.shape[1] // 2
    cos_t = rope_table[:, :pair_count]
    sin_t = rope_table[:, pair_count:]
    queries = apply_rotary(qkv_all[:, :, :group], cos_t[:, None, None], sin_t[:, None, None]).astype(jnp.bfloat16)
    new_k = apply_rotary(qkv_all[:, :, group], cos_t[:, None], sin_t[:, None]).astype(jnp.bfloat16)
    new_v = qkv_all[:, :, group + 1].astype(jnp.bfloat16)
    return x_f32, queries, new_k, new_v


def local_step(x, k_cache, v_cache, rope_table, norm_gain, w_qkv, b_qkv, w_out):
    kv_local, head_dim = k_cache.shape[1], k_cache.shape[2]
    tok_rows = x.shape[0]
    x_f32, queries, new_k, new_v = project_new(x, rope_table, norm_gain, w_qkv, b_qkv, kv_local, head_dim)
    group = queries.shape[2]
    k_prefix = lax.all_gather(k_cache, 'cp')
    v_prefix = lax.all_gather(v_cache, 'cp')
    k_recent = lax.all_gather(new_k, 'cp')
    v_recent = lax.all_gather(new_v, 'cp')
    cp_size = k_prefix.shape[0]
    scale = head_dim ** -0.5
    q_pos = lax.axis_index('cp') * tok_rows + jnp.arange(tok_rows)

    def attend(carry, block):
        run_max, run_sum, weighted = carry
        kp_block, vp_block, kr_block, vr_block, source = block
        s_pref = jnp.einsum('tngd,knd->tngk', queries, kp_block, preferred_element_type=jnp.float32) * scale
        s_recent = jnp.einsum('tngd,knd->tngk', queries, kr_block, preferred_element_type=jnp.float32) * scale
        k_pos = source * tok_rows + jnp.arange(tok_rows)
        visible = (k_pos[None, :] <= q_pos[:, None])[:, None, None, :]
        s_recent = jnp.where(visible, s_recent, MASK_VALUE)
        new_max = jnp.maximum(run_max, jnp.maximum(s_pref.max(axis=-1), s_recent.max(axis=-1)))
        rescale = jnp.exp(run_max - new_max)
        p_pref = jnp.exp(s_pref - new_max[..., None])
        p_recent = jnp.exp(s_recent - new_max[..., None])
        run_sum = run_sum * rescale + p_pref.sum(axis=-1) + p_recent.sum(axis=-1)
        weighted = (weighted * rescale[..., None]
                    + jnp.einsum('tngk,knd->tngd', p_pref.astype(jnp.bfloat16), vp_block, preferred_element_type=jnp.float32)
                    + jnp.einsum('tngk,knd->tngd', p_recent.astype(jnp.bfloat16), vr_block, preferred_element_type=jnp.float32))
        return (new_max, run_sum, weighted), None

    stat_shape = (tok_rows, kv_local, group)
    start_carry = (jnp.full(stat_shape, MASK_VALUE, jnp.float32), jnp.zeros(stat_shape, jnp.float32), jnp.zeros(stat_shape + (head_dim,), jnp.float32))
    (run_max, run_sum, weighted), _ = lax.scan(attend, start_carry, (k_prefix, v_prefix, k_recent, v_recent, jnp.arange(cp_size)))
    attn = (weighted / run_sum[..., None]).astype(jnp.bfloat16).reshape(tok_rows, kv_local * group * head_dim)
    proj_part = jnp.dot(attn, w_out, preferred_element_type=jnp.float32)
    y = (x_f32 + lax.psum(proj_part, 'tp')).astype(jnp.bfloat16)
    return y, new_k, new_v


def solution(mesh):
    row_spec = P(('dp', 'cp'), None)
    cache_spec = P(('dp', 'cp'), 'tp', None)
    return jax.shard_map(local_step, mesh=mesh, in_specs=(row_spec, cache_spec, cache_spec, row_spec, P(None), P(None, 'tp'), P('tp'), P('tp', None)), out_specs=(row_spec, cache_spec, cache_spec), check_vma=False)
```

profile of v0, /device:TPU:1, one launch (start us, length us, event | category | flops | bytes accessed | tf_op | source)
XLA Modules:
  0.0 1049.8 jit_solution(12590041715586053892)
XLA Ops:
  10.7 13.1 %convolution_add_fusion = f32[256,2304]{1,0:T(8,128)} fusion(bf16[4096,2304]{1,0:T(8,128)(2,1)} %param.15, bf16[256,4096]{1,0:T(8,128)(2,1)} %param.10, f32[4096]{0:T(1024)S(1)} %convert_element_type.74, f32[256]{0:T(256)S(1)} %add_rsqrt_fusion, f32[2304]{0:T(1024)S(1)} %convert_element_type.76), kind=kOutput, calls=%fused_computation.55 | convolution fusion | flops 4836622336 | bytes 23357440 | tf_op jit(solution)/shard_map/dot_general | solution.py:26
  36.5 66.2 %all-gather.14.cloned.1.call-done = bf16[16384,1,1,128]{0,3,2,1:T(8,128)(2,1)} async-done(((bf16[256,1,1,128]{0,3,2,1:T(8,128)(2,1)}), bf16[16384,1,1,128]{0,3,2,1:T(8,128)(2,1)}) %all-gather.14.cloned.1.call-update) | async-done | bytes 4194320 | tf_op jit(solution)/shard_map/all_gather | solution.py:45
  102.7 3.4 copy.58
  106.1 4.3 copy.49
  110.5 63.7 %all-gather.10.cloned.1.call-done = bf16[16384,1,128]{2,0,1:T(8,128)(2,1)} async-done(((bf16[256,1,128]{2,0,1:T(8,128)(2,1)}), bf16[16384,1,128]{2,0,1:T(8,128)(2,1)}) %all-gather.10.cloned.1.call-update) | async-done | bytes 4194320 | tf_op jit(solution)/shard_map/all_gather | solution.py:42
  174.2 68.9 %all-gather.12.cloned.1.call-done = bf16[16384,1,128]{2,0,1:T(8,128)(2,1)} async-done(((bf16[256,1,128]{2,0,1:T(8,128)(2,1)}), bf16[16384,1,128]{2,0,1:T(8,128)(2,1)}) %all-gather.12.cloned.1.call-update) | async-done | bytes 4194320 | tf_op jit(solution)/shard_map/all_gather | solution.py:43
  243.1 69.3 %all-gather.8.cloned.1.call-done = bf16[64,256,1,128]{3,1,2,0:T(8,128)(2,1)} async-done(((bf16[1,256,1,128]{3,1,2,0:T(8,128)(2,1)}), bf16[64,256,1,128]{3,1,2,0:T(8,128)(2,1)}) %all-gather.8.cloned.1.call-update) | async-done | bytes 4194320 | tf_op jit(solution)/shard_map/all_gather | solution.py:44
  312.4 683.4 %while.15 = (s32[]{:T(128)}, f32[256,1,16]{0,2,1:T(8,128)S(1)}, f32[256,1,16]{0,2,1:T(8,128)S(1)}, f32[256,1,16,128]{0,3,2,1:T(8,128)S(1)}, bf16[64,256,1,128]{3...) while((s32[]{:T(128)}, f32[256,1,16]{0,2,1:T(8,128)S(1)}, ...), condition=%wide.region_6.7_spmd.clone, body=%wide.region_1.6_spmd.clone.sunk | while | flops 1095852544 | bytes 36524232 | solution.py:70
  320.6 2.4 bitcast_add_fusion.7
  331.3 2.4 bitcast_add_fusion.7
  342.0 2.4 bitcast_add_fusion.7
  352.7 2.4 bitcast_add_fusion.7
  363.3 2.4 bitcast_add_fusion.7
  374.0 2.4 bitcast_add_fusion.7
  395.4 2.4 bitcast_add_fusion.7
  406.0 2.4 bitcast_add_fusion.7
  416.7 2.4 bitcast_add_fusion.7
  438.1 2.4 bitcast_add_fusion.7
  448.8 2.4 bitcast_add_fusion.7
  459.4 2.4 bitcast_add_fusion.7
  480.8 2.4 bitcast_add_fusion.7
  996.0 10.2 fusion.55
  1008.8 30.4 %all-reduce.2.cloned.1.call-done = f32[256,4096]{1,0:T(8,128)} async-done(((f32[256,4096]{1,0:T(8,128)}), f32[256,4096]{1,0:T(8,128)}) %all-reduce.2.cloned.1.call-update) | async-done | bytes 4194320 | tf_op jit(solution)/shard_map/psum | solution.py:73
  1039.2 4.1 fusion.45
  (746 shorter events, 623.4 us)
Async XLA Ops:
  7.2 95.6 %all-gather.14.cloned.1.call-start = ((), (), s32[]{:S(2)}) async-start(), calls=%async_computation.4 | async-start | bytes 4259840 | tf_op jit(solution)/shard_map/all_gather | solution.py:45
  23.8 4.5 copy-start.3
  25.9 3.4 copy-start.1
  26.6 147.6 %all-gather.10.cloned.1.call-start = ((), (), s32[]{:S(2)}) async-start(), calls=%async_computation.2 | async-start | bytes 4259840 | tf_op jit(solution)/shard_map/all_gather | solution.py:42
  27.4 215.7 %all-gather.12.cloned.1.call-start = ((), (), s32[]{:S(2)}) async-start(), calls=%async_computation.3 | async-start | bytes 4259840 | tf_op jit(solution)/shard_map/all_gather | solution.py:43
  28.1 284.3 %all-gather.8.cloned.1.call-start = ((), (), s32[]{:S(2)}) async-start(), calls=%async_computation | async-start | bytes 4259840 | tf_op jit(solution)/shard_map/all_gather | solution.py:44
  29.2 1010.0 %all-reduce.2.cloned.1.call-start = ((), (), s32[]{:S(2)}) async-start(), calls=%async_computation.1 | async-start | bytes 8388608 | tf_op jit(solution)/shard_map/psum | solution.py:73
  32.7 1.1 copy-start.2
  1006.2 33.0 %copy-start = (bf16[256,4096]{1,0:T(8,128)(2,1)S(1)}, bf16[256,4096]{1,0:T(8,128)(2,1)}, u32[]{:S(2)}) copy-start(bf16[256,4096]{1,0:T(8,128)(2,1)} %param.10) | copy-start | bytes 6291460
Sparse Core Ops, SparseCore 0:
  26.8 75.9 all-gather.13
  105.6 68.5 all-gather.9
  177.1 65.9 all-gather.11
  246.4 65.9 all-gather.7
  1006.3 32.7 all-reduce.1
where the time goes:
time: 1060 us; the launch traced here: 1050 us
  matrix products  510 us (48%)
  waiting for transfers between devices  300 us (28%)
  other arithmetic  121 us (11%)
  local copies, waits for them, and re-layouts  57.7 us (5%)
  loops' own time  47 us (4%)
  between operations  14 us (1%)
    dot_general x64, matrix products, attend(): jnp.einsum('tngk,knd->tngd', p_pref.astype(jnp.bfloat16), vp_block, prefe...  156 us
    dot_general x64, matrix products, attend(): jnp.einsum('tngk,knd->tngd', p_recent.astype(jnp.bfloat16), vr_block, pre...  129 us
    dot_general x64, matrix products, attend(): jnp.einsum('tngd,knd->tngk', queries, kr_block, preferred_element_type=jn...  103 us
    reduce_sum x64, other arithmetic, attend(): run_sum = run_sum * rescale + p_pref.sum(axis=-1) + p_recent.sum(axis=-1)  103 us
    dot_general x64, matrix products, attend(): jnp.einsum('tngd,knd->tngk', queries, kp_block, preferred_element_type=jn...  99.8 us
    all_gather x1, waiting for transfers between devices, local_step(): k_recent = lax.all_gather(new_k, 'cp')  69.3 us
    all_gather x1, waiting for transfers between devices, local_step(): v_prefix = lax.all_gather(v_cache, 'cp')  68.9 us
    all_gather x1, waiting for transfers between devices, local_step(): v_recent = lax.all_gather(new_v, 'cp')  66.2 us
  transfers between devices with their start and end apart: 5, of which 5 were waited for; matrix products, arithmetic and copies ran while one was open for 2% of the time, Pallas kernels for 0%

commit v1 on v0

v1 whole, which is shorter than its diff:
```python
import functools
import jax
import jax.numpy as jnp
from jax import lax
from jax.experimental import pallas as pl
from jax.experimental.pallas import tpu as pltpu
from jax.sharding import PartitionSpec as P

EPS = 1.5625e-07
MASK_VALUE = -1e30
LOG2E = 1.4426950408889634
f32 = jnp.float32
bf16 = jnp.bfloat16
HEADS = 16
ROWS = 256
HEAD = 128
HALF = 128
SCALE2 = HEAD ** -0.5 * LOG2E
U = 4
ORDERS = (("x", "y", "z"), ("y", "z", "x"), ("x", "z", "y"), ("x", "y", "z"))
SUBS = 4
WIDE = 512


def proj_kernel(x_ref, g_ref, cf_ref, sf_ref, w_ref, b_ref, q_ref, k_ref, v_ref, own_ref, h_ref):
    step = pl.program_id(0)

    @pl.when(step == 0)
    def _():
        xf = x_ref[...].astype(f32)
        inv = lax.rsqrt(jnp.mean(xf * xf, axis=-1, keepdims=True) + EPS)
        h_ref[...] = (xf * inv * g_ref[...].astype(f32)).astype(bf16)

    a = jnp.dot(h_ref[...], w_ref[...], preferred_element_type=f32) + b_ref[...].astype(f32)
    lane = lax.broadcasted_iota(jnp.int32, (ROWS, HEAD), 1)

    def rope(v):
        other = jnp.where(lane % 2 == 0, pltpu.roll(v, HEAD - 1, 1), pltpu.roll(v, 1, 1))
        return v * cf_ref[...] + other * sf_ref[...]

    @pl.when(step < 8)
    def _():
        for i in range(2):
            q_ref[0, :, i * ROWS:(i + 1) * ROWS] = rope(a[:, i * HEAD:(i + 1) * HEAD]).T.astype(bf16)

    @pl.when(step == 8)
    def _():
        k = rope(a[:, :HEAD]).astype(bf16)
        v = a[:, HEAD:]
        k_ref[...] = k
        v_ref[...] = v.astype(bf16)
        vt = v.T.astype(bf16)
        for i in range(2):
            own_ref[i, 0] = k[i * HALF:(i + 1) * HALF]
            own_ref[i, 1] = vt[:, i * HALF:(i + 1) * HALF]


def project(x, norm_gain, cf, sf, w_qkv, b_qkv):
    const = lambda *shape: pl.BlockSpec(shape, lambda s: (0,) * len(shape))
    return pl.pallas_call(
        proj_kernel,
        grid=(9,),
        in_specs=[const(ROWS, 4096), const(1, 4096), const(ROWS, HEAD), const(ROWS, HEAD),
                  pl.BlockSpec((4096, 256), lambda s: (0, s)), pl.BlockSpec((1, 256), lambda s: (0, s))],
        out_specs=[pl.BlockSpec((1, HEAD, WIDE), lambda s: (jnp.minimum(s, 7), 0, 0)), const(ROWS, HEAD), const(ROWS, HEAD),
                   const(2, 2, HALF, HEAD)],
        out_shape=[jax.ShapeDtypeStruct((8, HEAD, WIDE), bf16), jax.ShapeDtypeStruct((ROWS, HEAD), bf16),
                   jax.ShapeDtypeStruct((ROWS, HEAD), bf16), jax.ShapeDtypeStruct((2, 2, HALF, HEAD), bf16)],
        scratch_shapes=[pltpu.VMEM((ROWS, 4096), bf16)],
        compiler_params=pltpu.CompilerParams(vmem_limit_bytes=48 * 2 ** 20),
        name="project",
    )(x, norm_gain.reshape(1, -1), cf, sf, w_qkv, b_qkv.reshape(1, -1))


def attn_kernel(q_ref, ownc_ref, ownn_ref, out_ref, buf, qw, acc, m, l, s, p, osend, orecv,
                snd, rcv, loc, qsem, osem):
    r = lax.axis_index("cp")
    div, rem = lax.div, lax.rem
    me = {"z": div(r, 16), "y": rem(div(r, 4), 4), "x": rem(r, 4)}
    partner = 63 - r

    def rank_of(axis, d):
        c = dict(me)
        c[axis] = rem(me[axis] + d, 4)
        return c["z"] * 16 + c["y"] * 4 + c["x"]

    def remote(src, dst, ss, rs, rank):
        return pltpu.make_async_remote_copy(src_ref=src, dst_ref=dst, send_sem=ss, recv_sem=rs, device_id={"cp": rank},
                                            device_id_type=pl.DeviceIdType.MESH)

    peers = [rank_of(a, d) for a in "xyz" for d in (1, 3)] + [rank_of("x", 2), rank_of("y", 2), partner]
    barrier = pltpu.get_barrier_semaphore()
    for peer in peers:
        pl.semaphore_signal(barrier, inc=1, device_id={"cp": peer}, device_id_type=pl.DeviceIdType.MESH)

    def place(u, c1, c2, c3):
        return 64 * u + c3 * 16 + c2 * 4 + c1

    def own_place(u):
        return buf.at[place(u, *(me[a] for a in ORDERS[u]))]

    def own_src(u):
        return ownc_ref.at[u] if u < 2 else ownn_ref.at[u - 2]

    local = [pltpu.make_async_copy(own_src(u), own_place(u), loc.at[u]) for u in range(4)]
    for c in local:
        c.start()
    qw[pl.ds(0, 4)] = q_ref[pl.ds(0, 4)]
    acc[...] = jnp.zeros_like(acc)
    l[...] = jnp.zeros_like(l)
    m[...] = jnp.full_like(m, MASK_VALUE)
    for c in local:
        c.wait()
    pl.semaphore_wait(barrier, len(peers))

    def copies(u, phase, step):
        a1, a2, a3 = ORDERS[u]
        c1, c2, c3 = (me[a] for a in ORDERS[u])
        if phase == 1:
            return [(own_src(u), own_place(u), buf.at[place(u, rem(c1 + 4 - d, 4), c2, c3)], rank_of(a1, d), n)
                    for n, d in enumerate((1, 3, 2))]
        size, axis, tag = (4, a2, 3) if phase == 2 else (16, a3, 7)

        def group(off, part=None):
            first = place(u, 0, rem(c2 + off, 4), c3) if phase == 2 else place(u, 0, 0, rem(c3 + off, 4))
            if part is None:
                return buf.at[pl.ds(first, size)]
            return buf.at[pl.ds(first + part * (size // 2), size // 2)]

        if step == 1:
            return [(group(0), group(0), group(3), rank_of(axis, 1), tag),
                    (group(0), group(0), group(1), rank_of(axis, 3), tag + 1)]
        return [(group(3, 0), group(3, 0), group(2, 0), rank_of(axis, 1), tag + 2),
                (group(1, 1), group(1, 1), group(2, 1), rank_of(axis, 3), tag + 3)]

    def start(units, phase, step=1):
        for u in units:
            for src, dst, _, rank, tag in copies(u, phase, step):
                remote(src, dst, snd.at[u, tag], rcv.at[u, tag], rank).start()

    def arrived(units, phase, step=1):
        for u in units:
            for src, dst, got, rank, tag in copies(u, phase, step):
                remote(got, got, snd.at[u, tag], rcv.at[u, tag], rank).wait_recv()

    def sent(units, phase, step=1):
        for u in units:
            for src, dst, got, rank, tag in copies(u, phase, step):
                remote(src, dst, snd.at[u, tag], rcv.at[u, tag], rank).wait_send()

    cache, new = (0, 1), (2, 3)
    start(cache, 1)
    q_copy = remote(q_ref.at[pl.ds(4, 4)], qw.at[pl.ds(4, 4)], qsem.at[0], qsem.at[1], partner)
    q_copy.start()
    arrived(cache, 1)
    start(cache, 2, 1)
    arrived(cache, 2, 1)
    start(cache, 2, 2)
    start(new, 1)
    arrived(cache, 2, 2)
    start(cache, 3, 1)
    q_copy.wait()

    def event(b):
        @pl.when(b == 2)
        def _():
            arrived(new, 1)
            start(new, 2, 1)

        @pl.when(b == 7)
        def _():
            arrived(cache, 3, 1)
            start(cache, 3, 2)
            arrived(new, 2, 1)
            start(new, 2, 2)

        @pl.when(b == 12)
        def _():
            arrived(new, 2, 2)
            start(new, 3, 1)

        @pl.when(b == 22)
        def _():
            arrived(new, 3, 1)
            start(new, 3, 2)

        @pl.when(b == 23)
        def _():
            arrived(cache, 3, 2)

        @pl.when(b == 27)
        def _():
            arrived(new, 3, 2)

    def cache_desc(chunk, prb):
        g, cg = div(chunk, 4), rem(chunk, 4)
        off = g + jnp.where(g == 2, 1, 0) - jnp.where(g == 3, 1, 0)
        plane = rem(jnp.where(cg < 2, me["z"], me["x"]) + off, 4)
        base = plane * 16 + jnp.where(cg < 2, 0, 64) + rem(cg, 2) * 8
        return base, base + 1, jnp.int32(2), prb

    def new_desc(c, prb):
        return 128 + rem(c, 4) * 16 + div(c, 4) * 4, 192 + 4 * c, jnp.int32(1), prb

    def pick(cond, a, b):
        return tuple(lax.select(cond, i, j) for i, j in zip(a, b))

    def desc_first(b):
        c1 = cache_desc(div(b, 2), 4 * rem(b, 2))
        c2 = cache_desc(12 + (b - 24), jnp.int32(4))
        c3 = new_desc(b - 28, jnp.int32(4))
        return pick(b < 24, c1, pick(b < 28, c2, c3))

    def desc_second(b):
        return pick(b < 4, cache_desc(12 + b, jnp.int32(0)), new_desc(b - 4, jnp.int32(0)))

    def scores(d, u, i, mx, mask):
        kk = jnp.concatenate([buf[d[0] + i * d[2], 0], buf[d[1] + i * d[2], 0]], axis=0)
        st = jnp.dot(kk, qw[d[3] + u], preferred_element_type=f32)
        if mask is not None:
            st = jnp.where(mask(i), st, MASK_VALUE)
        s[i * 256:(i + 1) * 256, :] = st
        t = jnp.max(st.reshape(32, 8, WIDE), axis=0)
        return t if mx is None else jnp.maximum(mx, t)

    def run(desc, bodies, mask=None, on_body=None):
        def at(b):
            return desc(jnp.minimum(b, bodies - 1))

        def step(d, dn, u, mx8):
            pr = d[3] + u
            nxt, un = (d, u + 1) if u + 1 < U else (dn, 0)
            mx = jnp.max(mx8, axis=0, keepdims=True) * SCALE2
            mo = m[pr]
            mn = jnp.maximum(mo, mx)
            alpha = jnp.exp2(mo - mn)
            m[pr] = mn
            ls = l[pr] * alpha
            weighted, mxn = None, None
            for i in range(SUBS):
                e = jnp.exp2(s[i * 256:(i + 1) * 256, :] * SCALE2 - mn)
                ls = ls + jnp.sum(e.reshape(32, 8, WIDE), axis=0)
                p[i % 2] = e.astype(bf16)
                mxn = scores(nxt, un, i, mxn, mask)
                vv = jnp.concatenate([buf[d[0] + i * d[2], 1], buf[d[1] + i * d[2], 1]], axis=1)
                part = jnp.dot(vv, p[i % 2], preferred_element_type=f32)
                weighted = part if weighted is None else weighted + part
            l[pr] = ls
            acc[pr] = acc[pr] * alpha + weighted
            return mxn

        d0 = at(jnp.int32(0))
        mx = None
        for i in range(SUBS):
            mx = scores(d0, 0, i, mx, mask)

        def body(b, mx):
            if on_body is not None:
                on_body(b)
            d, dn = at(b), at(b + 1)
            for u in range(U):
                mx = step(d, dn, u, mx)
            return mx

        lax.fori_loop(0, bodies, body, mx)

    def diagonal(rank, prb):
        c = div(rank, SUBS)

        def mask(i):
            key = (SUBS * c + i) * ROWS + lax.broadcasted_iota(jnp.int32, (256, WIDE), 0)
            return key <= rank * ROWS + (lax.broadcasted_iota(jnp.int32, (256, WIDE), 1) & (ROWS - 1))

        run(lambda b: new_desc(c, jnp.int32(prb)), 1, mask)

    def result(pr):
        return (acc[pr] / jnp.sum(l[pr], axis=0, keepdims=True)).astype(bf16)

    run(desc_first, 28 + div(partner, SUBS), on_body=event)
    diagonal(partner, 4)
    for h in range(4):
        osend[h] = result(4 + h)
    o_copy = remote(osend, orecv, osem.at[0], osem.at[1], partner)
    o_copy.start()
    run(desc_second, 4 + div(r, SUBS))
    diagonal(r, 0)
    for h in range(4):
        res = result(h)
        for q in range(2):
            out_ref[2 * h + q] = res[:, q * ROWS:(q + 1) * ROWS]
    o_copy.wait()
    for h in range(4):
        for q in range(2):
            out_ref[8 + 2 * h + q] = orecv[h, :, q * ROWS:(q + 1) * ROWS]

    for units in (cache, new):
        sent(units, 1)
        for phase in (2, 3):
            for step in (1, 2):
                sent(units, phase, step)


def attend(q, own_cache, own_new):
    vm = pl.BlockSpec(memory_space=pltpu.VMEM)
    return pl.pallas_call(
        attn_kernel,
        out_shape=jax.ShapeDtypeStruct((HEADS, HEAD, ROWS), bf16),
        in_specs=[vm] * 3,
        out_specs=vm,
        scratch_shapes=[
            pltpu.VMEM((256, 2, HALF, HEAD), bf16),
            pltpu.VMEM((8, HEAD, WIDE), bf16),
            pltpu.VMEM((8, HEAD, WIDE), f32),
            pltpu.VMEM((8, 1, WIDE), f32),
            pltpu.VMEM((8, 8, WIDE), f32),
            pltpu.VMEM((SUBS * 256, WIDE), f32),
            pltpu.VMEM((2, 256, WIDE), bf16),
            pltpu.VMEM((4, HEAD, WIDE), bf16),
            pltpu.VMEM((4, HEAD, WIDE), bf16),
            pltpu.SemaphoreType.DMA((4, 11)),
            pltpu.SemaphoreType.DMA((4, 11)),
            pltpu.SemaphoreType.DMA((4,)),
            pltpu.SemaphoreType.DMA((2,)),
            pltpu.SemaphoreType.DMA((2,)),
        ],
        compiler_params=pltpu.CompilerParams(collective_id=0, has_side_effects=True, vmem_limit_bytes=48 * 2 ** 20),
        name="attend",
    )(q, own_cache, own_new)


def local_step(x, k_cache, v_cache, rope_table, norm_gain, w_qkv, b_qkv, w_out):
    cos_t, sin_t = rope_table[:, :32], rope_table[:, 32:]
    cf = jnp.concatenate([jnp.repeat(cos_t, 2, axis=1), jnp.ones((ROWS, 64), f32)], axis=1)
    sf = jnp.concatenate([jnp.stack([-sin_t, sin_t], axis=-1).reshape(ROWS, 64), jnp.zeros((ROWS, 64), f32)], axis=1)
    q, new_k, new_v, own_new = project(x, norm_gain, cf, sf, w_qkv, b_qkv)
    kc = k_cache.reshape(2, HALF, HEAD)
    vc = v_cache.reshape(2, HALF, HEAD).transpose(0, 2, 1)
    own_cache = jnp.stack([kc, vc], axis=1)
    o_t = attend(q, own_cache, own_new)
    o = o_t.reshape(HEADS * HEAD, ROWS)
    x_f32 = x.astype(f32)
    parts = []
    for c in range(4):
        cols = slice(c * 1024, (c + 1) * 1024)
        part = lax.dot_general(o, w_out[:, cols], (((0,), (0,)), ((), ())), preferred_element_type=f32)
        other = lax.ppermute(part, "tp", [(0, 1), (1, 0)])
        parts.append((x_f32[:, cols] + (part + other)).astype(bf16))
    y = jnp.concatenate(parts, axis=1)
    return y, new_k.reshape(ROWS, 1, HEAD), new_v.reshape(ROWS, 1, HEAD)


def solution(mesh):
    row_spec = P(('dp', 'cp'), None)
    cache_spec = P(('dp', 'cp'), 'tp', None)
    step = jax.shard_map(local_step, mesh=mesh, in_specs=(row_spec, cache_spec, cache_spec, row_spec, P(None), P(None, 'tp'), P('tp'), P('tp', None)), out_specs=(row_spec, cache_spec, cache_spec), check_vma=False)

    def run(*args):
        with jax.sharding.use_abstract_mesh(mesh.abstract_mesh):
            return step(*args)
    return run
```

time: 1060 us -> 252 us (0.24)
  matrix products: 510 us -> 13.9 us
  waiting for transfers between devices: 300 us -> 2.06 us
  Pallas kernels: 0 us -> 217 us
  other arithmetic: 121 us -> 5.26 us
  local copies, waits for them, and re-layouts: 57.7 us -> 4.33 us
  loops' own time: 47 us -> 0 us
  between operations: 14 us -> 0.78 us
    dot_general x258 -> x4, matrix products: 510 us -> 13.9 us  [local_step(): lax.dot_general(o, w_out[:, cols], (((0,), (0,)), ((), ())), preferred_el...]
    all_gather x4 -> x0, waiting for transfers between devices: 268 us -> none  [the longest x1 69.3 us: local_step(): k_recent = lax.all_gather(new_k, 'cp')]
    pallas_call x0 -> x2, Pallas kernels: none -> 217 us  [the longest x1 202 us: attend(): pl.pallas_call(attn_kernel, out_shape=jax.ShapeDtypeStruct((HEADS, HEAD,...]
    reduce_sum x65 -> x0, other arithmetic: 105 us -> none  [the longest x64 103 us: attend(): run_sum = run_sum * rescale + p_pref.sum(axis=-1) + p_recent.sum(axis=-1)]
    another operation x1 -> x0, loops' own time: 47 us -> none  [local_step(): lax.scan(attend, start_carry, (k_prefix, v_prefix, k_recent, v_recent, jn...]
    dynamic_slice x64 -> x0, local copies, waits for them, and re-layouts: 37.7 us -> none  [local_step(): lax.scan(attend, start_carry, (k_prefix, v_prefix, k_recent, v_recent, jn...]
    psum x1 -> x0, waiting for transfers between devices: 30.4 us -> none  [local_step(): y = (x_f32 + lax.psum(proj_part, 'tp')).astype(jnp.bfloat16)]
  transfers between devices with their start and end apart: 5 -> 4, of which waited for: 5 -> 1; matrix products, arithmetic and copies ran while one was open for 2% -> 4% of each run, Pallas kernels for 0% -> 0%
where the time goes in v1:
time: 252 us
  Pallas kernels  217 us (86%)
  matrix products  13.9 us (6%)
  starting transfers between devices  7.9 us (3%)
  other arithmetic  5.26 us (2%)
  local copies, waits for them, and re-layouts  4.33 us (2%)
    pallas_call x1, Pallas kernels, attend(): pl.pallas_call(attn_kernel, out_shape=jax.ShapeDtypeStruct((HEADS, HEAD,...  202 us
    pallas_call x1, Pallas kernels, project(): pl.pallas_call(proj_kernel, grid=(9,), in_specs=[const(ROWS, 4096), const...  14.9 us
    dot_general x4, matrix products, local_step(): lax.dot_general(o, w_out[:, cols], (((0,), (0,)), ((), ())), preferred_el...  13.9 us
    ppermute x4, starting transfers between devices, local_step(): other = lax.ppermute(part, 'tp', [(0, 1), (1, 0)])  7.9 us
  transfers between devices with their start and end apart: 4, of which 1 were waited for; matrix products, arithmetic and copies ran while one was open for 4% of the time, Pallas kernels for 0%

profile of v1, /device:TPU:1, one launch (start us, length us, event | category | flops | bytes accessed | tf_op | source)
XLA Modules:
  0.0 251.6 jit_solution(8461147485898703104)
XLA Ops:
  0.6 0.7 reshape.33.b_ref
  1.3 0.7 reshape.30.g_ref
  2.0 1.0 copy.16
  3.0 0.8 negate_bitcast_fusion
  3.8 0.1 copy.14
  3.9 0.1 copy.15
  4.1 0.1 copy.13
  4.2 0.9 pad_maximum_fusion.1.ownc_ref
  5.1 0.0 copy-start
  5.1 1.6 copy-done
  6.7 14.9 %project.1 = (bf16[8,128,512]{2,1,0:T(8,128)(2,1)S(1)}, bf16[256,128]{1,0:T(8,128)(2,1)}, bf16[256,128]{1,0:T(8,128)(2,1)}, bf16[2,2,128,128]{3,2,1,0:T(8,128)(2,1)S(1)}) custom-call(bf16[256,4096]{1,0:T(8,128)(2,1)S(1)} %copy-done, bf16[1,4096]{1,0:T(2,128)(2,1)S(1)} %reshape.30.g_ref, f32[256,128]{1,0:T(8,128)S(1)} %concatenate.9.cf_ref, ...), custom_call_target="tpu_custom_call" | custom-call | tf_op jit(solution)/shard_map/project/pallas_call | solution.py:60
  21.6 202.5 %attend.1 = bf16[16,128,256]{2,1,0:T(8,128)(2,1)S(1)} custom-call(bf16[8,128,512]{2,1,0:T(8,128)(2,1)S(1)} %get-tuple-element.7.q_ref, bf16[2,2,128,128]{3,2,1,0:T(8,128)(2,1)S(1)} %pad_maximum_fusion.1.ownc_ref, bf16[2,2,128,128]{3,2,1,0:T(8,128)(2,1)S(1)} %get-tuple-element.8.ownn_ref), custom_call_target="tpu_custom_call" | custom-call | tf_op jit(solution)/shard_map/attend/pallas_call | solution.py:305
  224.1 3.5 %fusion.6 = f32[256,1024]{1,0:T(8,128)S(1)} fusion(bf16[2048,256]{1,0:T(8,128)(2,1)S(1)} %bitcast.20, bf16[2048,4096]{1,0:T(8,128)(2,1)} %param.15), kind=kOutput, calls=%fused_computation.6 | convolution fusion | flops 1073741824 | bytes 6291456 | tf_op jit(solution)/shard_map/dot_general | solution.py:345
  227.6 7.1 %collective-permute-start = (f32[256,1024]{1,0:T(8,128)S(1)}, f32[256,1024]{1,0:T(8,128)S(1)}, u32[]{:S(2)}, u32[]{:S(2)}) collective-permute-start(f32[256,1024]{1,0:T(8,128)S(1)} %fusion.6), channel_id=1, source_target_pairs={{0,64},{64,0},{1,65},{65,1},{2,66},{66,2},{3,67},{67,3},{4,68},{68... | collective-permute-start | bytes 3145736 | tf_op jit(solution)/shard_map/ppermute | solution.py:346
  234.6 3.5 %fusion.4 = f32[256,1024]{1,0:T(8,128)S(1)} fusion(bf16[2048,256]{1,0:T(8,128)(2,1)S(1)} %bitcast.21, bf16[2048,4096]{1,0:T(8,128)(2,1)} %param.15), kind=kOutput, calls=%fused_computation.4 | convolution fusion | flops 1073741824 | bytes 6291456 | tf_op jit(solution)/shard_map/dot_general | solution.py:345
  238.1 0.1 collective-permute-start.1
  238.2 3.5 %fusion.2 = f32[256,1024]{1,0:T(8,128)S(1)} fusion(bf16[2048,256]{1,0:T(8,128)(2,1)S(1)} %bitcast.22, bf16[2048,4096]{1,0:T(8,128)(2,1)} %param.15), kind=kOutput, calls=%fused_computation.2 | convolution fusion | flops 1073741824 | bytes 6291456 | tf_op jit(solution)/shard_map/dot_general | solution.py:345
  241.7 0.6 collective-permute-start.2
  242.2 3.5 %fusion = f32[256,1024]{1,0:T(8,128)S(1)} fusion(bf16[2048,256]{1,0:T(8,128)(2,1)S(1)} %bitcast.23, bf16[2048,4096]{1,0:T(8,128)(2,1)} %param.15), kind=kOutput, calls=%fused_computation | convolution fusion | flops 1073741824 | bytes 6291456 | tf_op jit(solution)/shard_map/dot_general | solution.py:345
  245.8 0.2 collective-permute-start.3
  245.9 0.5 convert_element_type.15
  246.4 2.0 collective-permute-done.3
  248.5 1.6 fusion.11
  250.1 1.5 pad_maximum_fusion
  (11 shorter events, 0.2 us)
Async XLA Ops:
  5.1 1.6 copy-start
  227.6 18.8 %collective-permute-start = (f32[256,1024]{1,0:T(8,128)S(1)}, f32[256,1024]{1,0:T(8,128)S(1)}, u32[]{:S(2)}, u32[]{:S(2)}) collective-permute-start(f32[256,1024]{1,0:T(8,128)S(1)} %fusion.6), channel_id=1, source_target_pairs={{0,64},{64,0},{1,65},{65,1},{2,66},{66,2},{3,67},{67,3},{4,68},{68... | collective-permute-start | bytes 3145736 | tf_op jit(solution)/shard_map/ppermute | solution.py:346
  238.1 8.3 %collective-permute-start.1 = (f32[256,1024]{1,0:T(8,128)S(1)}, f32[256,1024]{1,0:T(8,128)S(1)}, u32[]{:S(2)}, u32[]{:S(2)}) collective-permute-start(f32[256,1024]{1,0:T(8,128)S(1)} %fusion.4), channel_id=1, source_target_pairs={{0,64},{64,0},{1,65},{65,1},{2,66},{66,2},{3,67},{67,3},{4,68},{68... | collective-permute-start | bytes 3145736 | tf_op jit(solution)/shard_map/ppermute | solution.py:346
  241.7 4.3 %copy-start.1 = (bf16[256,4096]{1,0:T(8,128)(2,1)S(1)}, bf16[256,4096]{1,0:T(8,128)(2,1)}, u32[]{:S(2)}) copy-start(bf16[256,4096]{1,0:T(8,128)(2,1)} %x_ref.1) | copy-start | bytes 6291460
  241.7 4.8 %collective-permute-start.2 = (f32[256,1024]{1,0:T(8,128)S(1)}, f32[256,1024]{1,0:T(8,128)S(1)}, u32[]{:S(2)}, u32[]{:S(2)}) collective-permute-start(f32[256,1024]{1,0:T(8,128)S(1)} %fusion.2), channel_id=1, source_target_pairs={{0,64},{64,0},{1,65},{65,1},{2,66},{66,2},{3,67},{67,3},{4,68},{68... | collective-permute-start | bytes 3145736 | tf_op jit(solution)/shard_map/ppermute | solution.py:346
  245.8 2.7 %collective-permute-start.3 = (f32[256,1024]{1,0:T(8,128)S(1)}, f32[256,1024]{1,0:T(8,128)S(1)}, u32[]{:S(2)}, u32[]{:S(2)}) collective-permute-start(f32[256,1024]{1,0:T(8,128)S(1)} %fusion), channel_id=1, source_target_pairs={{0,64},{64,0},{1,65},{65,1},{2,66},{66,2},{3,67},{67,3},{4,68},{68... | collective-permute-start | bytes 3145736 | tf_op jit(solution)/shard_map/ppermute | solution.py:346

commit v2 on v1

--- a/solution.py
+++ b/solution.py
@@ -127,11 +127,16 @@
                 return buf.at[pl.ds(first, size)]
             return buf.at[pl.ds(first + part * (size // 2), size // 2)]
 
-        if step == 1:
-            return [(group(0), group(0), group(3), rank_of(axis, 1), tag),
-                    (group(0), group(0), group(1), rank_of(axis, 3), tag + 1)]
-        return [(group(3, 0), group(3, 0), group(2, 0), rank_of(axis, 1), tag + 2),
-                (group(1, 1), group(1, 1), group(2, 1), rank_of(axis, 3), tag + 3)]
+        up, down = rank_of(axis, 1), rank_of(axis, 3)
+        if step == 1 and phase == 2:
+            return [(group(0), group(0), group(3), up, tag), (group(0), group(0), group(1), down, tag + 1)]
+        if step < 2:
+            h = int(2 * step)
+            return [(group(0, h), group(0, h), group(3, h), up, tag + 2 * h),
+                    (group(0, h), group(0, h), group(1, h), down, tag + 2 * h + 1)]
+        out = [(group(3, 0), group(3, 0), group(2, 0), up, tag + 2 + size // 8),
+               (group(1, 1), group(1, 1), group(2, 1), down, tag + 3 + size // 8)]
+        return out if step == 2 else [out[int(step) - 3]]
 
     def start(units, phase, step=1):
         for u in units:
@@ -149,64 +154,72 @@
                 remote(src, dst, snd.at[u, tag], rcv.at[u, tag], rank).wait_send()
 
     cache, new = (0, 1), (2, 3)
+    q_copy = remote(q_ref.at[pl.ds(4, 4)], qw.at[pl.ds(4, 4)], qsem.at[0], qsem.at[1], partner)
     start(cache, 1)
-    q_copy = remote(q_ref.at[pl.ds(4, 4)], qw.at[pl.ds(4, 4)], qsem.at[0], qsem.at[1], partner)
     q_copy.start()
     arrived(cache, 1)
     start(cache, 2, 1)
+    start(new, 1)
     arrived(cache, 2, 1)
     start(cache, 2, 2)
-    start(new, 1)
+    arrived(new, 1)
+    start(new, 2, 1)
     arrived(cache, 2, 2)
-    start(cache, 3, 1)
-    q_copy.wait()
-
-    def event(b):
-        @pl.when(b == 2)
-        def _():
-            arrived(new, 1)
-            start(new, 2, 1)
-
-        @pl.when(b == 7)
-        def _():
-            arrived(cache, 3, 1)
-            start(cache, 3, 2)
+    start(cache, 3, 0)
+    start(cache, 3, 0.5)
+
+    def event(at):
+        @pl.when(at == 3)
+        def _():
+            q_copy.wait()
             arrived(new, 2, 1)
             start(new, 2, 2)
 
-        @pl.when(b == 12)
+        @pl.when(at == 7)
+        def _():
+            arrived(cache, 3, 0)
+            start(cache, 3, 3)
+
+        @pl.when(at == 8)
         def _():
             arrived(new, 2, 2)
-            start(new, 3, 1)
-
-        @pl.when(b == 22)
-        def _():
-            arrived(new, 3, 1)
+            start(new, 3, 0)
+            start(new, 3, 0.5)
+
+        @pl.when(at == 15)
+        def _():
+            arrived(cache, 3, 0.5)
+            start(cache, 3, 4)
+
+        @pl.when(at == 23)
+        def _():
+            arrived(cache, 3, 2)
+            arrived(new, 3, 0)
+            arrived(new, 3, 0.5)
             start(new, 3, 2)
 
-        @pl.when(b == 23)
-        def _():
-            arrived(cache, 3, 2)
-
-        @pl.when(b == 27)
+        @pl.when(at == 27)
         def _():
             arrived(new, 3, 2)
 
     def cache_desc(chunk, prb):
         g, cg = div(chunk, 4), rem(chunk, 4)
-        off = g + jnp.where(g == 2, 1, 0) - jnp.where(g == 3, 1, 0)
+        second = rem(cg, 2)
+        near = (g == 1) | (g == 2)
+        off = jnp.where(near, 1 + 2 * second, jnp.where(g == 0, 0, 2))
+        half = jnp.where(near, g - 1, second)
         plane = rem(jnp.where(cg < 2, me["z"], me["x"]) + off, 4)
-        base = plane * 16 + jnp.where(cg < 2, 0, 64) + rem(cg, 2) * 8
-        return base, base + 1, jnp.int32(2), prb
+        base = plane * 16 + jnp.where(cg < 2, 0, 64) + half * 8
+        return base, base + 4, prb
 
     def new_desc(c, prb):
-        return 128 + rem(c, 4) * 16 + div(c, 4) * 4, 192 + 4 * c, jnp.int32(1), prb
+        return 128 + rem(c, 4) * 16 + div(c, 4) * 4, 192 + 4 * c, prb
 
     def pick(cond, a, b):
         return tuple(lax.select(cond, i, j) for i, j in zip(a, b))
 
     def desc_first(b):
-        c1 = cache_desc(div(b, 2), 4 * rem(b, 2))
+        c1 = cache_desc(4 * div(b, 8) + rem(b, 4), 4 * rem(div(b, 4), 2))
         c2 = cache_desc(12 + (b - 24), jnp.int32(4))
         c3 = new_desc(b - 28, jnp.int32(4))
         return pick(b < 24, c1, pick(b < 28, c2, c3))
@@ -214,97 +227,121 @@
     def desc_second(b):
         return pick(b < 4, cache_desc(12 + b, jnp.int32(0)), new_desc(b - 4, jnp.int32(0)))
 
-    def scores(d, u, i, mx, mask):
-        kk = jnp.concatenate([buf[d[0] + i * d[2], 0], buf[d[1] + i * d[2], 0]], axis=0)
-        st = jnp.dot(kk, qw[d[3] + u], preferred_element_type=f32)
-        if mask is not None:
-            st = jnp.where(mask(i), st, MASK_VALUE)
+    def desc_of(turn, b):
+        return pick(turn == 0, desc_first(b), desc_second(b))
+
+    def scores(d, u, i, mx):
+        run4, j = buf.at[pl.ds(d[i // 2], 4)], 2 * (i % 2)
+        kk = jnp.concatenate([run4[j, 0], run4[j + 1, 0]], axis=0)
+        st = jnp.dot(kk, qw[d[2] + u], preferred_element_type=f32)
         s[i * 256:(i + 1) * 256, :] = st
         t = jnp.max(st.reshape(32, 8, WIDE), axis=0)
         return t if mx is None else jnp.maximum(mx, t)
 
-    def run(desc, bodies, mask=None, on_body=None):
-        def at(b):
-            return desc(jnp.minimum(b, bodies - 1))
-
-        def step(d, dn, u, mx8):
-            pr = d[3] + u
-            nxt, un = (d, u + 1) if u + 1 < U else (dn, 0)
-            mx = jnp.max(mx8, axis=0, keepdims=True) * SCALE2
+    def step(d, dn, u, mx8):
+        pr = d[2] + u
+        nxt, un = (d, u + 1) if u + 1 < U else (dn, 0)
+        mx = jnp.max(mx8, axis=0, keepdims=True) * SCALE2
+        mo = m[pr]
+        mn = jnp.maximum(mo, mx)
+        alpha = jnp.exp2(mo - mn)
+        m[pr] = mn
+        ls = l[pr] * alpha
+        weighted, mxn = None, None
+        for i in range(SUBS):
+            e = jnp.exp2(s[i * 256:(i + 1) * 256, :] * SCALE2 - mn)
+            ls = ls + jnp.sum(e.reshape(32, 8, WIDE), axis=0)
+            p[i % 2] = e.astype(bf16)
+            mxn = scores(nxt, un, i, mxn)
+            run4, j = buf.at[pl.ds(d[i // 2], 4)], 2 * (i % 2)
+            vv = jnp.concatenate([run4[j, 1], run4[j + 1, 1]], axis=1)
+            part = jnp.dot(vv, p[i % 2], preferred_element_type=f32)
+            weighted = part if weighted is None else weighted + part
+        l[pr] = ls
+        acc[pr] = acc[pr] * alpha + weighted
+        return mxn
+
+    def masked_block(rank, prb, block):
+        f = 128 + rem(div(block, 4), 4) * 16 + div(block, 16) * 4 + rem(block, 4)
+        g = 192 + block
+        key = block * ROWS + lax.broadcasted_iota(jnp.int32, (256, WIDE), 0)
+        seen = key <= rank * ROWS + (lax.broadcasted_iota(jnp.int32, (256, WIDE), 1) & (ROWS - 1))
+        kk = jnp.concatenate([buf[f, 0], buf[g, 0]], axis=0)
+        vv = jnp.concatenate([buf[f, 1], buf[g, 1]], axis=1)
+        for u in range(4):
+            pr = prb + u
+            st = jnp.where(seen, jnp.dot(kk, qw[pr], preferred_element_type=f32), MASK_VALUE)
+            mx = jnp.max(jnp.max(st.reshape(32, 8, WIDE), axis=0), axis=0, keepdims=True) * SCALE2
             mo = m[pr]
             mn = jnp.maximum(mo, mx)
             alpha = jnp.exp2(mo - mn)
             m[pr] = mn
-            ls = l[pr] * alpha
-            weighted, mxn = None, None
-            for i in range(SUBS):
-                e = jnp.exp2(s[i * 256:(i + 1) * 256, :] * SCALE2 - mn)
-                ls = ls + jnp.sum(e.reshape(32, 8, WIDE), axis=0)
-                p[i % 2] = e.astype(bf16)
-                mxn = scores(nxt, un, i, mxn, mask)
-                vv = jnp.concatenate([buf[d[0] + i * d[2], 1], buf[d[1] + i * d[2], 1]], axis=1)
-                part = jnp.dot(vv, p[i % 2], preferred_element_type=f32)
-                weighted = part if weighted is None else weighted + part
-            l[pr] = ls
-            acc[pr] = acc[pr] * alpha + weighted
-            return mxn
-
-        d0 = at(jnp.int32(0))
+            e = jnp.exp2(st * SCALE2 - mn)
+            l[pr] = l[pr] * alpha + jnp.sum(e.reshape(32, 8, WIDE), axis=0)
+            acc[pr] = acc[pr] * alpha + jnp.dot(vv, e.astype(bf16), preferred_element_type=f32)
+
+    o_copy = remote(osend, orecv, osem.at[0], osem.at[1], partner)
+
+    def turn_body(turn, carry):
+        rank = lax.select(turn == 0, partner, r)
+        bodies = lax.select(turn == 0, jnp.int32(28), jnp.int32(4)) + div(rank, SUBS)
+        prb = lax.select(turn == 0, jnp.int32(4), jnp.int32(0))
+        d0 = desc_of(turn, jnp.int32(0))
         mx = None
         for i in range(SUBS):
-            mx = scores(d0, 0, i, mx, mask)
+            mx = scores(d0, 0, i, mx)
 
         def body(b, mx):
-            if on_body is not None:
-                on_body(b)
-            d, dn = at(b), at(b + 1)
+            event(b + 1000 * turn)
+            d, dn = desc_of(turn, b), desc_of(turn, jnp.minimum(b + 1, bodies - 1))
             for u in range(U):
                 mx = step(d, dn, u, mx)
             return mx
 
         lax.fori_loop(0, bodies, body, mx)
-
-    def diagonal(rank, prb):
-        c = div(rank, SUBS)
-
-        def mask(i):
-            key = (SUBS * c + i) * ROWS + lax.broadcasted_iota(jnp.int32, (256, WIDE), 0)
-            return key <= rank * ROWS + (lax.broadcasted_iota(jnp.int32, (256, WIDE), 1) & (ROWS - 1))
-
-        run(lambda b: new_desc(c, jnp.int32(prb)), 1, mask)
-
-    def result(pr):
-        return (acc[pr] / jnp.sum(l[pr], axis=0, keepdims=True)).astype(bf16)
-
-    run(desc_first, 28 + div(partner, SUBS), on_body=event)
-    diagonal(partner, 4)
-    for h in range(4):
-        osend[h] = result(4 + h)
-    o_copy = remote(osend, orecv, osem.at[0], osem.at[1], partner)
-    o_copy.start()
-    run(desc_second, 4 + div(r, SUBS))
-    diagonal(r, 0)
-    for h in range(4):
-        res = result(h)
-        for q in range(2):
-            out_ref[2 * h + q] = res[:, q * ROWS:(q + 1) * ROWS]
+        start_block = rank - rem(rank, SUBS)
+
+        def tail(j, carry):
+            masked_block(rank, prb, start_block + j)
+            return carry
+
+        lax.fori_loop(0, rem(rank, SUBS) + 1, tail, 0)
+
+        def result(h, carry):
+            res = (acc[prb + h] / jnp.sum(l[prb + h], axis=0, keepdims=True)).T.astype(bf16)
+
+            @pl.when(turn == 0)
+            def _():
+                osend[h] = res
+
+            @pl.when(turn == 1)
+            def _():
+                out_ref[h] = res
+
+            return carry
+
+        lax.fori_loop(0, 4, result, 0)
+
+        @pl.when(turn == 0)
+        def _():
+            o_copy.start()
+
+        return carry
+
+    lax.fori_loop(0, 2, turn_body, 0)
     o_copy.wait()
-    for h in range(4):
-        for q in range(2):
-            out_ref[8 + 2 * h + q] = orecv[h, :, q * ROWS:(q + 1) * ROWS]
+    out_ref[pl.ds(4, 4)] = orecv[...]
 
     for units in (cache, new):
-        sent(units, 1)
-        for phase in (2, 3):
-            for step in (1, 2):
-                sent(units, phase, step)
+        for phase, step in ((1, 1), (2, 1), (2, 2), (3, 0), (3, 0.5), (3, 2)):
+            sent(units, phase, step)
 
 
 def attend(q, own_cache, own_new):
     vm = pl.BlockSpec(memory_space=pltpu.VMEM)
     return pl.pallas_call(
         attn_kernel,
-        out_shape=jax.ShapeDtypeStruct((HEADS, HEAD, ROWS), bf16),
+        out_shape=jax.ShapeDtypeStruct((8, WIDE, HEAD), bf16),
         in_specs=[vm] * 3,
         out_specs=vm,
         scratch_shapes=[
@@ -315,10 +352,10 @@
             pltpu.VMEM((8, 8, WIDE), f32),
             pltpu.VMEM((SUBS * 256, WIDE), f32),
             pltpu.VMEM((2, 256, WIDE), bf16),
-            pltpu.VMEM((4, HEAD, WIDE), bf16),
-            pltpu.VMEM((4, HEAD, WIDE), bf16),
-            pltpu.SemaphoreType.DMA((4, 11)),
-            pltpu.SemaphoreType.DMA((4, 11)),
+            pltpu.VMEM((4, WIDE, HEAD), bf16),
+            pltpu.VMEM((4, WIDE, HEAD), bf16),
+            pltpu.SemaphoreType.DMA((4, 13)),
+            pltpu.SemaphoreType.DMA((4, 13)),
             pltpu.SemaphoreType.DMA((4,)),
             pltpu.SemaphoreType.DMA((2,)),
             pltpu.SemaphoreType.DMA((2,)),
@@ -326,6 +363,54 @@
         compiler_params=pltpu.CompilerParams(collective_id=0, has_side_effects=True, vmem_limit_bytes=48 * 2 ** 20),
         name="attend",
     )(q, own_cache, own_new)
+
+
+TILE = 512
+TILES = 4096 // TILE
+
+
+def out_kernel(o_ref, w_ref, x_ref, y_ref, o_s, mine, other, snd, rcv):
+    step = pl.program_id(0)
+    peer = 1 - lax.axis_index("tp")
+
+    def copy(j):
+        return pltpu.make_async_remote_copy(src_ref=mine.at[j], dst_ref=other.at[j], send_sem=snd.at[j], recv_sem=rcv.at[j],
+                                            device_id={"tp": peer}, device_id_type=pl.DeviceIdType.MESH)
+
+    @pl.when(step == 0)
+    def _():
+        barrier = pltpu.get_barrier_semaphore()
+        pl.semaphore_signal(barrier, inc=1, device_id={"tp": peer}, device_id_type=pl.DeviceIdType.MESH)
+        for h in range(HEADS):
+            o_s[:, h * HEAD:(h + 1) * HEAD] = o_ref[h // 2, (h % 2) * ROWS:(h % 2 + 1) * ROWS, :]
+        pl.semaphore_wait(barrier, 1)
+
+    @pl.when(step < TILES)
+    def _():
+        mine[step] = jnp.dot(o_s[...], w_ref[...], preferred_element_type=f32)
+        copy(step).start()
+
+    @pl.when(step > 0)
+    def _():
+        copy(step - 1).wait()
+        y_ref[...] = (x_ref[...].astype(f32) + (mine[step - 1] + other[step - 1])).astype(bf16)
+
+
+def out_project(o, w_out, x):
+    late = lambda j: (0, jnp.maximum(j - 1, 0))
+    return pl.pallas_call(
+        out_kernel,
+        grid=(TILES + 1,),
+        in_specs=[pl.BlockSpec((8, WIDE, HEAD), lambda j: (0, 0, 0)),
+                  pl.BlockSpec((HEADS * HEAD, TILE), lambda j: (0, jnp.minimum(j, TILES - 1))),
+                  pl.BlockSpec((ROWS, TILE), late)],
+        out_specs=pl.BlockSpec((ROWS, TILE), late),
+        out_shape=jax.ShapeDtypeStruct((ROWS, 4096), bf16),
+        scratch_shapes=[pltpu.VMEM((ROWS, HEADS * HEAD), bf16), pltpu.VMEM((TILES, ROWS, TILE), f32),
+                        pltpu.VMEM((TILES, ROWS, TILE), f32), pltpu.SemaphoreType.DMA((TILES,)), pltpu.SemaphoreType.DMA((TILES,))],
+        compiler_params=pltpu.CompilerParams(collective_id=1, has_side_effects=True, vmem_limit_bytes=48 * 2 ** 20),
+        name="outproj",
+    )(o, w_out, x)
 
 
 def local_step(x, k_cache, v_cache, rope_table, norm_gain, w_qkv, b_qkv, w_out):
@@ -336,16 +421,8 @@
     kc = k_cache.reshape(2, HALF, HEAD)
     vc = v_cache.reshape(2, HALF, HEAD).transpose(0, 2, 1)
     own_cache = jnp.stack([kc, vc], axis=1)
-    o_t = attend(q, own_cache, own_new)
-    o = o_t.reshape(HEADS * HEAD, ROWS)
-    x_f32 = x.astype(f32)
-    parts = []
-    for c in range(4):
-        cols = slice(c * 1024, (c + 1) * 1024)
-        part = lax.dot_general(o, w_out[:, cols], (((0,), (0,)), ((), ())), preferred_element_type=f32)
-        other = lax.ppermute(part, "tp", [(0, 1), (1, 0)])
-        parts.append((x_f32[:, cols] + (part + other)).astype(bf16))
-    y = jnp.concatenate(parts, axis=1)
+    o = attend(q, own_cache, own_new)
+    y = out_project(o, w_out, x)
     return y, new_k.reshape(ROWS, 1, HEAD), new_v.reshape(ROWS, 1, HEAD)
 
 

time: 252 us -> 219 us (0.87)
  matrix products: 13.9 us -> 0 us
  starting transfers between devices: 7.9 us -> 0 us
  Pallas kernels: 217 us -> 212 us
  other arithmetic: 5.26 us -> 1.65 us
    dot_general x4 -> x0, matrix products: 13.9 us -> none  [local_step(): lax.dot_general(o, w_out[:, cols], (((0,), (0,)), ((), ())), preferred_el...]
    ppermute x4 -> x0, starting transfers between devices: 7.9 us -> none  [local_step(): other = lax.ppermute(part, 'tp', [(0, 1), (1, 0)])]
    pallas_call x1 -> x2, Pallas kernels: 202 us -> 197 us  [the longest x1 180 us: attend(): pl.pallas_call(attn_kernel, out_shape=jax.ShapeDtypeStruct((8, WIDE, HEAD...]
  transfers between devices with their start and end apart: 4 -> 0, of which waited for: 1 -> 0; matrix products, arithmetic and copies ran while one was open for 4% -> 0% of each run, Pallas kernels for 0% -> 0%
where the time goes in v2:
time: 219 us; the launch traced here: 218 us
  Pallas kernels  212 us (97%)
  local copies, waits for them, and re-layouts  4.22 us (2%)
    pallas_call x1, Pallas kernels, attend(): pl.pallas_call(attn_kernel, out_shape=jax.ShapeDtypeStruct((8, WIDE, HEAD...  180 us
    pallas_call x1, Pallas kernels, out_project(): pl.pallas_call(out_kernel, grid=(TILES + 1,), in_specs=[pl.BlockSpec((8,...  16.4 us
    pallas_call x1, Pallas kernels, project(): pl.pallas_call(proj_kernel, grid=(9,), in_specs=[const(ROWS, 4096), const...  14.9 us

profile of v2, /device:TPU:1, one launch (start us, length us, event | category | flops | bytes accessed | tf_op | source)
XLA Modules:
  0.0 218.2 jit_solution(17242329670700625644)
XLA Ops:
  0.6 0.0 copy-start
  0.6 0.8 reshape.30.b_ref
  1.5 0.7 reshape.27.g_ref
  2.2 1.0 copy.16
  3.2 0.9 pad_maximum_fusion.ownc_ref
  4.0 0.8 negate_bitcast_fusion
  4.8 0.1 copy.14
  4.9 0.1 copy.15
  5.1 0.1 copy.13
  5.3 0.0 copy-done
  5.3 14.9 %project.1 = (bf16[8,128,512]{2,1,0:T(8,128)(2,1)S(1)}, bf16[256,128]{1,0:T(8,128)(2,1)}, bf16[256,128]{1,0:T(8,128)(2,1)}, bf16[2,2,128,128]{3,2,1,0:T(8,128)(2,1)S(1)}) custom-call(bf16[256,4096]{1,0:T(8,128)(2,1)S(1)} %copy-done, bf16[1,4096]{1,0:T(2,128)(2,1)S(1)} %reshape.27.g_ref, f32[256,128]{1,0:T(8,128)S(1)} %concatenate.6.cf_ref, ...), custom_call_target="tpu_custom_call" | custom-call | tf_op jit(solution)/shard_map/project/pallas_call | solution.py:60
  20.2 180.3 %attend.1.o_ref = bf16[8,512,128]{2,1,0:T(8,128)(2,1)S(1)} custom-call(bf16[8,128,512]{2,1,0:T(8,128)(2,1)S(1)} %get-tuple-element.7.q_ref, bf16[2,2,128,128]{3,2,1,0:T(8,128)(2,1)S(1)} %pad_maximum_fusion.ownc_ref, bf16[2,2,128,128]{3,2,1,0:T(8,128)(2,1)S(1)} %get-tuple-element.8.ownn_ref), custom_call_target="tpu_custom_call" | custom-call | tf_op jit(solution)/shard_map/attend/pallas_call | solution.py:342
  200.5 16.4 %outproj.1 = bf16[256,4096]{1,0:T(8,128)(2,1)S(1)} custom-call(bf16[8,512,128]{2,1,0:T(8,128)(2,1)S(1)} %attend.1.o_ref, bf16[2048,4096]{1,0:T(8,128)(2,1)} %w_ref.3, bf16[256,4096]{1,0:T(8,128)(2,1)S(1)} %copy-done), custom_call_target="tpu_custom_call" | custom-call | tf_op jit(solution)/shard_map/outproj/pallas_call | solution.py:401
  216.9 1.3 copy.18
  (6 shorter events, 0.2 us)
Async XLA Ops:
  0.6 4.6 %copy-start = (bf16[256,4096]{1,0:T(8,128)(2,1)S(1)}, bf16[256,4096]{1,0:T(8,128)(2,1)}, u32[]{:S(2)}) copy-start(bf16[256,4096]{1,0:T(8,128)(2,1)} %x_ref.3) | copy-start | bytes 6291460

commit v3 on v2

--- a/solution.py
+++ b/solution.py
@@ -191,12 +191,19 @@
             arrived(cache, 3, 0.5)
             start(cache, 3, 4)
 
+        @pl.when(at == 18)
+        def _():
+            arrived(new, 3, 0)
+            start(new, 3, 3)
+
+        @pl.when(at == 21)
+        def _():
+            arrived(new, 3, 0.5)
+            start(new, 3, 4)
+
         @pl.when(at == 23)
         def _():
             arrived(cache, 3, 2)
-            arrived(new, 3, 0)
-            arrived(new, 3, 0.5)
-            start(new, 3, 2)
 
         @pl.when(at == 27)
         def _():

time: 219 us -> 216 us (0.986)
  Pallas kernels: 212 us -> 209 us
    pallas_call x1, Pallas kernels: 180 us -> 177 us  [attend(): pl.pallas_call(attn_kernel, out_shape=jax.ShapeDtypeStruct((8, WIDE, HEAD...]
where the time goes in v3:
time: 216 us
  Pallas kernels  209 us (97%)
  local copies, waits for them, and re-layouts  4.22 us (2%)
    pallas_call x1, Pallas kernels, attend(): pl.pallas_call(attn_kernel, out_shape=jax.ShapeDtypeStruct((8, WIDE, HEAD...  177 us
    pallas_call x1, Pallas kernels, out_project(): pl.pallas_call(out_kernel, grid=(TILES + 1,), in_specs=[pl.BlockSpec((8,...  16.6 us
    pallas_call x1, Pallas kernels, project(): pl.pallas_call(proj_kernel, grid=(9,), in_specs=[const(ROWS, 4096), const...  14.9 us

profile of v3, /device:TPU:1, one launch (start us, length us, event | category | flops | bytes accessed | tf_op | source)
XLA Modules:
  0.0 215.7 jit_solution(463329420418434307)
XLA Ops:
  0.6 0.0 copy-start
  0.6 0.8 reshape.30.b_ref
  1.5 0.7 reshape.27.g_ref
  2.2 1.0 copy.16
  3.2 0.9 pad_maximum_fusion.ownc_ref
  4.0 0.8 negate_bitcast_fusion
  4.8 0.1 copy.14
  4.9 0.1 copy.15
  5.1 0.1 copy.13
  5.3 0.0 copy-done
  5.3 14.9 %project.1 = (bf16[8,128,512]{2,1,0:T(8,128)(2,1)S(1)}, bf16[256,128]{1,0:T(8,128)(2,1)}, bf16[256,128]{1,0:T(8,128)(2,1)}, bf16[2,2,128,128]{3,2,1,0:T(8,128)(2,1)S(1)}) custom-call(bf16[256,4096]{1,0:T(8,128)(2,1)S(1)} %copy-done, bf16[1,4096]{1,0:T(2,128)(2,1)S(1)} %reshape.27.g_ref, f32[256,128]{1,0:T(8,128)S(1)} %concatenate.6.cf_ref, ...), custom_call_target="tpu_custom_call" | custom-call | tf_op jit(solution)/shard_map/project/pallas_call | solution.py:60
  20.2 177.5 %attend.1.o_ref = bf16[8,512,128]{2,1,0:T(8,128)(2,1)S(1)} custom-call(bf16[8,128,512]{2,1,0:T(8,128)(2,1)S(1)} %get-tuple-element.7.q_ref, bf16[2,2,128,128]{3,2,1,0:T(8,128)(2,1)S(1)} %pad_maximum_fusion.ownc_ref, bf16[2,2,128,128]{3,2,1,0:T(8,128)(2,1)S(1)} %get-tuple-element.8.ownn_ref), custom_call_target="tpu_custom_call" | custom-call | tf_op jit(solution)/shard_map/attend/pallas_call | solution.py:349
  197.7 16.6 %outproj.1 = bf16[256,4096]{1,0:T(8,128)(2,1)S(1)} custom-call(bf16[8,512,128]{2,1,0:T(8,128)(2,1)S(1)} %attend.1.o_ref, bf16[2048,4096]{1,0:T(8,128)(2,1)} %w_ref.3, bf16[256,4096]{1,0:T(8,128)(2,1)S(1)} %copy-done), custom_call_target="tpu_custom_call" | custom-call | tf_op jit(solution)/shard_map/outproj/pallas_call | solution.py:408
  214.3 1.3 copy.18
  (6 shorter events, 0.2 us)
Async XLA Ops:
  0.6 4.6 %copy-start = (bf16[256,4096]{1,0:T(8,128)(2,1)S(1)}, bf16[256,4096]{1,0:T(8,128)(2,1)}, u32[]{:S(2)}) copy-start(bf16[256,4096]{1,0:T(8,128)(2,1)} %x_ref.3) | copy-start | bytes 6291460
